TPU v7x, 32 devices: a whole 2x2x4 slice. The times are simulated.
32 devices in a mesh: io: 16 (over z, x, core), rep: 2 (over y).
Axes of the slice: x: 2, y: 2, z: 4, core: 2. Of those that a mesh axis runs over, the one named last changes fastest.
Arguments:
- snapshots: float32 [49152, 2048], P(('rep', 'io')), parts along dimension 0, may hold values from -6 to 6
Outputs:
- coefficients: float32 [32, 256, 2048], P('rep', None, 'io'), parts along dimension 0
- resid_var: float32 [512, 2048], P('rep', 'io'), parts along dimension 0
There are 2 independent parts, one for each index of `rep`. A program takes and returns all parts, laid end to end along the dimension named above; each array names one. Nothing has to cross between parts.
All inputs are finite; a program needn't handle non-finite values.
Results may differ from a plain program's by a relative error of at most 0.000071.
Values sent between devices are 32-bit elements; how exact they have to be, the bound alone decides.
A program may use at most 128 MiB of HBM per device.

v0:
```python
import jax
import jax.numpy as jnp
from jax import lax
from jax.sharding import PartitionSpec as P

TIMES = 96
HARM = 16


def basis_matrix(times):
    steps = jnp.arange(times).astype(jnp.float32)
    columns = [jnp.ones_like(steps), (steps - (times - 1) / 2.0) / (times / 2.0)]
    for harmonic in range(1, 7):
        columns.append(jnp.cos(2.0 * jnp.pi * harmonic * steps / 12.0))
    for harmonic in range(1, 6):
        columns.append(jnp.sin(2.0 * jnp.pi * harmonic * steps / 12.0))
    columns.append(jnp.cos(2.0 * jnp.pi * steps / times))
    columns.append(jnp.sin(2.0 * jnp.pi * steps / times))
    columns.append(jnp.cos(4.0 * jnp.pi * steps / times))
    return jnp.stack(columns, axis=1)


def projector_of(basis):
    gram = jnp.dot(basis.T, basis, precision=lax.Precision.HIGHEST)
    factor = jnp.linalg.cholesky(gram)
    middle = lax.linalg.triangular_solve(factor, basis.T, left_side=True, lower=True)
    return lax.linalg.triangular_solve(factor, middle, left_side=True, lower=True, transpose_a=True)


def fit_block(block, basis, projector):
    width = block.shape[-1]
    lat_rows = block.shape[0] // TIMES
    series = block.reshape(TIMES, lat_rows * width)
    coeffs = jnp.dot(projector, series, precision=lax.Precision.HIGHEST)
    moments = jnp.dot(basis.T, series, precision=lax.Precision.HIGHEST)
    total = jnp.sum(series * series, axis=0)
    variance = (total - jnp.sum(coeffs * moments, axis=0)) / TIMES
    return (coeffs.reshape(HARM, lat_rows, width), variance.reshape(1, lat_rows, width))


def local(snapshots):
    groups = lax.axis_size("io")
    local_rows = snapshots.shape[0]
    lon_dev = snapshots.shape[1] // groups
    split_view = snapshots.reshape(local_rows, groups, lon_dev)
    basis = basis_matrix(TIMES)
    projector = projector_of(basis)
    moved = lax.all_to_all(split_view, "io", split_axis=1, concat_axis=0, tiled=True)
    coeffs, variance = fit_block(moved[:, 0, :], basis, projector)
    return (coeffs, variance[0])


def solution(mesh):
    placed = (P(("rep", "io"), None),)
    return jax.shard_map(
        local,
        mesh=mesh,
        in_specs=placed,
        out_specs=(P("rep", None, "io"), P("rep", "io")),
        check_vma=False,
    )
```

profile of v0, /device:TPU:11, one launch (start us, length us, event | category | flops | bytes accessed | tf_op | source)
XLA Modules:
  0.0 326.1 jit_solution(2681641074615959106)
XLA Ops:
  0.6 10.3 %copy_bitcast_fusion = f32[1536,16,128]{2,0,1:T(8,128)} fusion(f32[1536,2048]{1,0:T(8,128)} %param.1), kind=kLoop, calls=%fused_computation.1 | loop fusion | bytes 25165824 | tf_op jit(solution)/shard_map/reshape | solution.py:45
  10.9 6.5 %all-to-all-start = ((f32[1536,16,128]{2,0,1:T(8,128)}), f32[1536,16,128]{2,0,1:T(8,128)}, u32[]{:S(2)}, u32[]{:S(2)}) async-start(f32[1536,16,128]{2,0,1:T(8,128)} %copy_bitcast_fusion), calls=%async_computation | async-start | bytes 25165824 | tf_op jit(solution)/shard_map/all_to_all | solution.py:48
  17.5 0.1 fusion.16
  17.6 0.1 fusion.14
  17.6 0.1 fusion.12
  17.7 0.1 fusion.10
  17.7 0.1 fusion.8
  17.8 0.1 multiply_cosine_fusion
  17.9 0.1 stack.2
  18.0 0.1 fusion.19
  18.1 0.1 copy.6
  18.2 1.5 cholesky.16
  19.7 0.6 compare_reduce_fusion
  20.3 0.6 fusion.1
  21.0 1.2 custom-call.8
  22.2 0.2 fusion.4
  22.4 0.1 fusion.2
  22.5 267.2 %all-to-all-done = f32[1536,16,128]{2,0,1:T(8,128)} async-done(((f32[1536,16,128]{2,0,1:T(8,128)}), f32[1536,16,128]{2,0,1:T(8,128)}, u32[]{:S(2)}, u32[]{:S(2)}) %all-to-all-start) | async-done | bytes 12582944 | tf_op jit(solution)/shard_map/all_to_all | solution.py:48
  289.7 13.8 %reshape_squeeze.3 = f32[96,32768]{1,0:T(8,128)} reshape(f32[16,1536,1,128]{3,1,0,2:T(8,128)} %bitcast.4) | data formatting | bytes 25165824 | tf_op jit(solution)/shard_map/reshape;squeeze | solution.py:33
  303.5 0.0 copy-start
  303.5 5.8 %multiply_reduce_fusion = f32[32768]{0:T(1024)S(1)} fusion(f32[96,32768]{1,0:T(8,128)} %reshape_squeeze.3), kind=kLoop, calls=%fused_computation.2 | loop fusion | flops 6258688 | bytes 12713984 | tf_op jit(solution)/shard_map/reduce_sum | solution.py:36
  309.3 2.4 copy-done
  311.7 6.0 %fusion.20 = f32[16,32768]{1,0:T(8,128)S(1)} fusion(f32[16,96]{1,0:T(8,128)S(1)} %fusion.2, f32[96,32768]{1,0:T(8,128)S(1)} %copy-done), kind=kOutput, calls=%fused_computation.39 | convolution fusion | flops 603979776 | bytes 14686208 | tf_op jit(solution)/shard_map/dot_general | solution.py:34
  317.6 6.1 %fusion = f32[32768]{0:T(1024)S(1)} fusion(f32[16,32768]{1,0:T(8,128)S(1)} %fusion.20, f32[96,16]{0,1:T(8,128)S(1)} %stack.2, f32[96,32768]{1,0:T(8,128)S(1)} %copy-done), kind=kOutput, calls=%fused_computation.3 | convolution fusion | flops 604995584 | bytes 14817280 | tf_op jit(solution)/shard_map/dot_general | solution.py:35
  323.7 1.7 copy.9
  325.4 0.7 multiply_bitcast_fusion
  (5 shorter events, 0.1 us)
Async XLA Ops:
  10.9 278.8 %all-to-all-start = ((f32[1536,16,128]{2,0,1:T(8,128)}), f32[1536,16,128]{2,0,1:T(8,128)}, u32[]{:S(2)}, u32[]{:S(2)}) async-start(f32[1536,16,128]{2,0,1:T(8,128)} %copy_bitcast_fusion), calls=%async_computation | async-start | bytes 25165824 | tf_op jit(solution)/shard_map/all_to_all | solution.py:48
  303.5 8.2 %copy-start = (f32[96,32768]{1,0:T(8,128)S(1)}, f32[96,32768]{1,0:T(8,128)}, u32[]{:S(2)}) copy-start(f32[96,32768]{1,0:T(8,128)} %reshape_squeeze.3) | copy-start | bytes 37748740
where the time goes:
time: 327 us; the launch traced here: 326 us
  waiting for transfers between devices  267 us (82%)
  local copies, waits for them, and re-layouts  28.3 us (9%)
  matrix products  12.5 us (4%)
  other arithmetic  10.9 us (3%)
  starting transfers between devices  6.52 us (2%)
    all_to_all x1, waiting for transfers between devices, local(): lax.all_to_all(split_view, 'io', split_axis=1, concat_axis=0, tiled=True)  267 us
    another operation x1, local copies, waits for them, and re-layouts, fit_block(): series = block.reshape(TIMES, lat_rows * width)  13.8 us
    reshape x1, local copies, waits for them, and re-layouts, local(): split_view = snapshots.reshape(local_rows, groups, lon_dev)  10.3 us
  transfers between devices with their start and end apart: 1, of which 1 were waited for; matrix products, arithmetic and copies ran while one was open for 2% of the time, Pallas kernels for 0%

commit v1 on v0

v1 whole, which is shorter than its diff:
```python
import functools

import jax
import jax.numpy as jnp
import numpy as np
from jax import lax
from jax.experimental import pallas as pl
from jax.experimental.pallas import tpu as pltpu
from jax.sharding import PartitionSpec as P

TIMES = 96
HARM = 16
MONTHS = 12
SPAN = 24
CHAIN = TIMES // SPAN
SLOW = 4
SUMS = MONTHS + SLOW + 1
LANES = 128
ROWS = 8
AHEAD = 8
MESH = pl.DeviceIdType.MESH


def fit_constants():
    steps = np.arange(TIMES, dtype=np.float64)
    slow = np.stack(
        [
            (steps - (TIMES - 1) / 2.0) / (TIMES / 2.0),
            np.cos(2.0 * np.pi * steps / TIMES),
            np.sin(2.0 * np.pi * steps / TIMES),
            np.cos(4.0 * np.pi * steps / TIMES),
        ],
        axis=1,
    )
    month = np.arange(MONTHS, dtype=np.float64)
    angles = 2.0 * np.pi * month / MONTHS
    periodic = [np.cos(j * angles) for j in range(7)] + [np.sin(j * angles) for j in range(1, 6)]
    unmix = np.linalg.inv(np.stack(periodic, axis=1))
    years = TIMES // MONTHS
    cross = slow.reshape(years, MONTHS, SLOW).sum(axis=0)
    inner = np.linalg.inv(slow.T @ slow - cross.T @ cross / years)
    return slow, cross, inner, unmix, years


def dot(weights, values):
    total = None
    for weight, value in zip(weights, values):
        term = value * np.float32(weight)
        total = term if total is None else total + term
    return total


def finish(sums):
    _, cross, inner, unmix, years = fit_constants()
    by_month, moments, squares = sums[:MONTHS], sums[MONTHS : MONTHS + SLOW], sums[-1]
    reduced = [moments[k] - dot(cross[:, k] / years, by_month) for k in range(SLOW)]
    slow = [dot(inner[k], reduced) for k in range(SLOW)]
    level = [(by_month[m] - dot(cross[m], slow)) * np.float32(1.0 / years) for m in range(MONTHS)]
    explained = slow[0] * moments[0]
    for k in range(1, SLOW):
        explained = explained + slow[k] * moments[k]
    for m in range(MONTHS):
        explained = explained + level[m] * by_month[m]
    half = MONTHS // 2
    even = [level[0]] + [level[m] + level[MONTHS - m] for m in range(1, half)] + [level[half]]
    odd = [level[m] - level[MONTHS - m] for m in range(1, half)]
    cosines = [dot(unmix[j, : half + 1], even) for j in range(half + 1)]
    sines = [dot(unmix[half + j, 1:half], odd) for j in range(1, half)]
    coeffs = [cosines[0], slow[0]] + cosines[1:] + sines + slow[1:]
    return coeffs, (squares - explained) * np.float32(1.0 / TIMES)


def kernel(
    groups, lat, local_rows,
    table, field, coeff_out, var_out,
    raw, part, below, above, done,
    raw_send, raw_recv, part_send, below_recv, above_recv, out_sem,
):
    members = groups // CHAIN
    chunks = lat // ROWS
    me = lax.axis_index("io")
    link, member = me // members, lax.rem(me, members)
    device = lambda at, who: {"io": at * members + who}

    barrier = pltpu.get_barrier_semaphore()
    for step in range(1, members):
        other = lax.rem(member + step, members)
        pl.semaphore_signal(barrier, inc=1, device_id=device(link, other), device_id_type=MESH)

    @pl.when(link > 0)
    def _():
        pl.semaphore_signal(barrier, inc=1, device_id=device(link - 1, member), device_id_type=MESH)

    @pl.when(link < CHAIN - 1)
    def _():
        pl.semaphore_signal(barrier, inc=1, device_id=device(link + 1, member), device_id_type=MESH)

    ends = (link == 0).astype(jnp.int32) + (link == CHAIN - 1).astype(jnp.int32)
    pl.semaphore_wait(barrier, members + 1 - ends)

    def spread_rows(chunk, row, count, time):
        for step in list(range(1, members)) + [0]:
            other = lax.rem(member + step, members)
            for to in range(CHAIN):
                lon = pl.multiple_of((to * members + other) * LANES, LANES)
                if count is None:
                    src = field.at[pl.ds(row, ROWS), pl.ds(lon, LANES)]
                    dst = raw.at[chunk, to, time]
                else:
                    src = field.at[:, pl.ds(row, ROWS), pl.ds(lon, LANES)]
                    dst = raw.at[chunk, to, pl.ds(time, count)]
                if step == 0:
                    pltpu.make_async_copy(src, dst, raw_recv.at[chunk]).start()
                else:
                    pltpu.make_async_remote_copy(
                        src_ref=src, dst_ref=dst, send_sem=raw_send, recv_sem=raw_recv.at[chunk],
                        device_id=device(link, other), device_id_type=MESH,
                    ).start()

    def spread(chunk):
        if local_rows % lat == 0:
            count = local_rows // lat
            spread_rows(chunk, pl.multiple_of(chunk * ROWS, ROWS), count, member * count)
        else:
            first = member * local_rows
            for extra in range(local_rows // lat + 2):
                time = first // lat + extra
                row = time * lat + chunk * ROWS - first

                @pl.when((row >= 0) & (row < local_rows))
                def _():
                    spread_rows(chunk, pl.multiple_of(row, ROWS), None, time)

    def send(chunk, to, up):
        pltpu.make_async_remote_copy(
            src_ref=part.at[chunk, to],
            dst_ref=(below if up else above).at[chunk, to],
            send_sem=part_send,
            recv_sem=(below_recv if up else above_recv).at[chunk, to],
            device_id=device(link + 1 if up else link - 1, member),
            device_id_type=MESH,
        ).start()

    def arrive(chunk, to, up):
        box, sem = (below, below_recv) if up else (above, above_recv)
        pltpu.make_async_copy(box.at[chunk, to], box.at[chunk, to], sem.at[chunk, to]).wait()
        for k in range(SUMS):
            part[chunk, to, k] = part[chunk, to, k] + box[chunk, to, k]

    def add_up(chunk):
        pltpu.make_async_copy(raw.at[chunk], raw.at[chunk], raw_recv.at[chunk]).wait()
        moments = [[None] * (SLOW + 1) for _ in range(CHAIN)]
        for month in range(MONTHS):
            kept = [None] * CHAIN
            for time in range(month, SPAN, MONTHS):
                weights = [table[(link * SPAN + time) * SLOW + k] for k in range(SLOW)]
                for to in range(CHAIN):
                    value = raw[chunk, to, time]
                    kept[to] = value if kept[to] is None else kept[to] + value
                    terms = [value * weight for weight in weights] + [value * value]
                    own = moments[to]
                    for k, term in enumerate(terms):
                        own[k] = term if own[k] is None else own[k] + term
            for to in range(CHAIN):
                part[chunk, to, month] = kept[to]
        for to in range(CHAIN):
            for k in range(SLOW + 1):
                part[chunk, to, MONTHS + k] = moments[to][k]

        @pl.when(link == 0)
        def _():
            for to in range(CHAIN - 1, 0, -1):
                send(chunk, to, True)

        @pl.when(link == CHAIN - 1)
        def _():
            for to in range(CHAIN - 1):
                send(chunk, to, False)

    def relay(step):
        for at in range(1, CHAIN - 1):

            @pl.when((link == at) & (step >= at) & (step < chunks + at))
            def _():
                for to in range(CHAIN - 1, at, -1):
                    arrive(step - at, to, True)
                    send(step - at, to, True)

            lag = CHAIN - 1 - at

            @pl.when((link == at) & (step >= lag) & (step < chunks + lag))
            def _():
                for to in range(at):
                    arrive(step - lag, to, False)
                    send(step - lag, to, False)

    def close(chunk):
        @pl.when(link > 0)
        def _():
            arrive(chunk, link, True)

        @pl.when(link < CHAIN - 1)
        def _():
            arrive(chunk, link, False)

        coeffs, variance = finish([part[chunk, link, k] for k in range(SUMS)])
        for k in range(HARM):
            done[chunk, k] = coeffs[k]
        done[chunk, HARM] = variance
        rows = pl.ds(pl.multiple_of(chunk * ROWS, ROWS), ROWS)
        pltpu.make_async_copy(done.at[chunk, pl.ds(0, HARM)], coeff_out.at[:, rows, :], out_sem.at[0]).start()
        pltpu.make_async_copy(done.at[chunk, HARM], var_out.at[rows, :], out_sem.at[1]).start()

    lag = CHAIN + 1
    lax.fori_loop(0, min(AHEAD, chunks), lambda c, _: (spread(c), 0)[1], 0)

    def body(step, carry):
        @pl.when(step + AHEAD < chunks)
        def _():
            spread(step + AHEAD)

        @pl.when(step < chunks)
        def _():
            add_up(step)

        relay(step)

        @pl.when(step >= lag)
        def _():
            close(step - lag)

        return carry

    lax.fori_loop(0, chunks + lag, body, 0)

    lons = pl.ds(0, (members - 1) * CHAIN * LANES)
    sent = field.at[:, :, lons] if local_rows % lat == 0 else field.at[:, lons]
    pltpu.make_async_copy(sent, sent, raw_send).wait()
    passed = part.at[:, pl.ds(0, CHAIN - 1)]
    pltpu.make_async_copy(passed, passed, part_send).wait()
    pltpu.make_async_copy(coeff_out, coeff_out, out_sem.at[0]).wait()
    pltpu.make_async_copy(var_out, var_out, out_sem.at[1]).wait()


def local(snapshots):
    groups = lax.axis_size("io")
    local_rows, width = snapshots.shape
    lat = local_rows * groups // TIMES
    if width != groups * LANES or lat % ROWS or local_rows % ROWS or groups % CHAIN:
        raise ValueError("unsupported sizes")
    chunks = lat // ROWS
    slow = fit_constants()[0]
    table = jnp.asarray(slow.reshape(-1), jnp.float32)
    field = snapshots.reshape(local_rows // lat, lat, width) if local_rows % lat == 0 else snapshots
    return pl.pallas_call(
        functools.partial(kernel, groups, lat, local_rows),
        out_shape=(
            jax.ShapeDtypeStruct((HARM, lat, LANES), jnp.float32),
            jax.ShapeDtypeStruct((lat, LANES), jnp.float32),
        ),
        in_specs=[pl.BlockSpec(memory_space=pltpu.SMEM), pl.BlockSpec(memory_space=pl.ANY)],
        out_specs=(pl.BlockSpec(memory_space=pl.ANY), pl.BlockSpec(memory_space=pl.ANY)),
        scratch_shapes=[
            pltpu.VMEM((chunks, CHAIN, SPAN, ROWS, LANES), jnp.float32),
            pltpu.VMEM((chunks, CHAIN, SUMS, ROWS, LANES), jnp.float32),
            pltpu.VMEM((chunks, CHAIN, SUMS, ROWS, LANES), jnp.float32),
            pltpu.VMEM((chunks, CHAIN, SUMS, ROWS, LANES), jnp.float32),
            pltpu.VMEM((chunks, SUMS, ROWS, LANES), jnp.float32),
            pltpu.SemaphoreType.DMA,
            pltpu.SemaphoreType.DMA((chunks,)),
            pltpu.SemaphoreType.DMA,
            pltpu.SemaphoreType.DMA((chunks, CHAIN)),
            pltpu.SemaphoreType.DMA((chunks, CHAIN)),
            pltpu.SemaphoreType.DMA((2,)),
        ],
        compiler_params=pltpu.CompilerParams(
            collective_id=0, has_side_effects=True, vmem_limit_bytes=56 * 2**20
        ),
        name="climatology",
    )(table, field)


def solution(mesh):
    return jax.shard_map(
        local,
        mesh=mesh,
        in_specs=(P(("rep", "io"), None),),
        out_specs=(P("rep", None, "io"), P("rep", "io")),
        check_vma=False,
    )
```

time: 327 us -> 167 us (0.51)
  waiting for transfers between devices: 267 us -> 0 us
  Pallas kernels: 0 us -> 159 us
  local copies, waits for them, and re-layouts: 28.3 us -> 3.81 us
  matrix products: 12.5 us -> 0 us
  other arithmetic: 10.9 us -> 0 us
  starting transfers between devices: 6.52 us -> 0 us
    all_to_all x1 -> x0, waiting for transfers between devices: 267 us -> none  [local(): lax.all_to_all(split_view, 'io', split_axis=1, concat_axis=0, tiled=True)]
    pallas_call x0 -> x1, Pallas kernels: none -> 159 us  [local(): pl.pallas_call(functools.partial(kernel, groups, lat, local_rows), out_sh...]
    another operation x3 -> x0, local copies, waits for them, and re-layouts: 13.9 us -> none  [the longest x1 13.8 us: fit_block(): series = block.reshape(TIMES, lat_rows * width)]
    dot_general x3 -> x0, matrix products: 12.2 us -> none  [the longest x1 6.06 us: fit_block(): moments = jnp.dot(basis.T, series, precision=lax.Precision.HIGHEST)]
    reshape x1 -> x0, local copies, waits for them, and re-layouts: 10.3 us -> none  [local(): split_view = snapshots.reshape(local_rows, groups, lon_dev)]
    all_to_all x1 -> x0, starting transfers between devices: 6.52 us -> none  [local(): lax.all_to_all(split_view, 'io', split_axis=1, concat_axis=0, tiled=True)]
    reduce_sum x1 -> x0, other arithmetic: 5.79 us -> none  [fit_block(): total = jnp.sum(series * series, axis=0)]
    another operation x5 -> x0, other arithmetic: 4.02 us -> none  [the longest x3 2.14 us: projector_of(): factor = jnp.linalg.cholesky(gram)]
  transfers between devices with their start and end apart: 1 -> 0, of which waited for: 1 -> 0; matrix products, arithmetic and copies ran while one was open for 2% -> 0% of each run, Pallas kernels for 0% -> 0%
where the time goes in v1:
time: 167 us; the launch traced here: 164 us
  Pallas kernels  159 us (95%)
  local copies, waits for them, and re-layouts  3.81 us (2%)
    pallas_call x1, Pallas kernels, local(): pl.pallas_call(functools.partial(kernel, groups, lat, local_rows), out_sh...  159 us
    unnamed x4, local copies, waits for them, and re-layouts  3.81 us

profile of v1, /device:TPU:11, one launch (start us, length us, event | category | flops | bytes accessed | tf_op | source)
XLA Modules:
  0.0 163.5 jit_solution(18241560211470876061)
XLA Ops:
  0.6 159.1 %climatology.1 = (f32[16,256,128]{2,1,0:T(8,128)}, f32[256,128]{1,0:T(8,128)}) custom-call(f32[384]{0:T(512)} %constant.2.clone.table, f32[6,256,2048]{2,1,0:T(8,128)} %bitcast.1), custom_call_target="tpu_custom_call" | custom-call | tf_op jit(solution)/shard_map/climatology/pallas_call | solution.py:255
  159.7 0.0 copy-start
  159.7 3.1 %copy.6 = f32[16,256,128]{2,1,0:T(8,128)} copy(f32[16,256,128]{2,1,0:T(8,128)} %get-tuple-element.4) | data formatting | bytes 4194304
  162.9 0.0 copy-done
  162.9 0.7 copy.7
Async XLA Ops:
  159.7 3.2 %copy-start = (f32[256,128]{1,0:T(8,128)S(1)}, f32[256,128]{1,0:T(8,128)}, u32[]{:S(2)}) copy-start(f32[256,128]{1,0:T(8,128)} %get-tuple-element.5) | copy-start | bytes 393220

commit v2 on v1

--- a/solution.py
+++ b/solution.py
@@ -18,6 +18,7 @@
 LANES = 128
 ROWS = 8
 AHEAD = 8
+CLOSE_LAG = 3
 MESH = pl.DeviceIdType.MESH
 
 
@@ -73,8 +74,8 @@
 def kernel(
     groups, lat, local_rows,
     table, field, coeff_out, var_out,
-    raw, part, below, above, done,
-    raw_send, raw_recv, part_send, below_recv, above_recv, out_sem,
+    raw, part, below, above,
+    raw_send, raw_recv, part_send, below_recv, above_recv,
 ):
     members = groups // CHAIN
     chunks = lat // ROWS
@@ -98,29 +99,35 @@
     ends = (link == 0).astype(jnp.int32) + (link == CHAIN - 1).astype(jnp.int32)
     pl.semaphore_wait(barrier, members + 1 - ends)
 
-    def spread_rows(chunk, row, count, time):
+    def block_at(rank):
+        orders = []
+        for at in range(CHAIN):
+            up, down = list(range(CHAIN - 1, at, -1)), list(range(at))
+            orders.append((up + down if len(up) >= len(down) else down + up) + [at])
+        return sum((link == at).astype(jnp.int32) * orders[at][rank] for at in range(CHAIN))
+
+    def spread_rows(chunk, to, row, count, time):
         for step in list(range(1, members)) + [0]:
             other = lax.rem(member + step, members)
-            for to in range(CHAIN):
-                lon = pl.multiple_of((to * members + other) * LANES, LANES)
-                if count is None:
-                    src = field.at[pl.ds(row, ROWS), pl.ds(lon, LANES)]
-                    dst = raw.at[chunk, to, time]
-                else:
-                    src = field.at[:, pl.ds(row, ROWS), pl.ds(lon, LANES)]
-                    dst = raw.at[chunk, to, pl.ds(time, count)]
-                if step == 0:
-                    pltpu.make_async_copy(src, dst, raw_recv.at[chunk]).start()
-                else:
-                    pltpu.make_async_remote_copy(
-                        src_ref=src, dst_ref=dst, send_sem=raw_send, recv_sem=raw_recv.at[chunk],
-                        device_id=device(link, other), device_id_type=MESH,
-                    ).start()
-
-    def spread(chunk):
+            lon = pl.multiple_of((to * members + other) * LANES, LANES)
+            if count is None:
+                src = field.at[pl.ds(row, ROWS), pl.ds(lon, LANES)]
+                dst = raw.at[chunk, to, time]
+            else:
+                src = field.at[:, pl.ds(row, ROWS), pl.ds(lon, LANES)]
+                dst = raw.at[chunk, to, pl.ds(time, count)]
+            if step == 0:
+                pltpu.make_async_copy(src, dst, raw_recv.at[chunk, to]).start()
+            else:
+                pltpu.make_async_remote_copy(
+                    src_ref=src, dst_ref=dst, send_sem=raw_send, recv_sem=raw_recv.at[chunk, to],
+                    device_id=device(link, other), device_id_type=MESH,
+                ).start()
+
+    def spread_block(chunk, to):
         if local_rows % lat == 0:
             count = local_rows // lat
-            spread_rows(chunk, pl.multiple_of(chunk * ROWS, ROWS), count, member * count)
+            spread_rows(chunk, to, pl.multiple_of(chunk * ROWS, ROWS), count, member * count)
         else:
             first = member * local_rows
             for extra in range(local_rows // lat + 2):
@@ -129,7 +136,14 @@
 
                 @pl.when((row >= 0) & (row < local_rows))
                 def _():
-                    spread_rows(chunk, pl.multiple_of(row, ROWS), None, time)
+                    spread_rows(chunk, to, pl.multiple_of(row, ROWS), None, time)
+
+    def each(step, act):
+        for rank in range(CHAIN):
+
+            @pl.when((step >= rank) & (step < chunks + rank))
+            def _():
+                act(step - rank, block_at(rank))
 
     def send(chunk, to, up):
         pltpu.make_async_remote_copy(
@@ -147,50 +161,43 @@
         for k in range(SUMS):
             part[chunk, to, k] = part[chunk, to, k] + box[chunk, to, k]
 
-    def add_up(chunk):
-        pltpu.make_async_copy(raw.at[chunk], raw.at[chunk], raw_recv.at[chunk]).wait()
-        moments = [[None] * (SLOW + 1) for _ in range(CHAIN)]
+    def add_up(chunk, to):
+        pltpu.make_async_copy(raw.at[chunk, to], raw.at[chunk, to], raw_recv.at[chunk, to]).wait()
+        moments = [None] * (SLOW + 1)
         for month in range(MONTHS):
-            kept = [None] * CHAIN
+            kept = None
             for time in range(month, SPAN, MONTHS):
-                weights = [table[(link * SPAN + time) * SLOW + k] for k in range(SLOW)]
-                for to in range(CHAIN):
-                    value = raw[chunk, to, time]
-                    kept[to] = value if kept[to] is None else kept[to] + value
-                    terms = [value * weight for weight in weights] + [value * value]
-                    own = moments[to]
-                    for k, term in enumerate(terms):
-                        own[k] = term if own[k] is None else own[k] + term
-            for to in range(CHAIN):
-                part[chunk, to, month] = kept[to]
-        for to in range(CHAIN):
-            for k in range(SLOW + 1):
-                part[chunk, to, MONTHS + k] = moments[to][k]
-
-        @pl.when(link == 0)
-        def _():
-            for to in range(CHAIN - 1, 0, -1):
-                send(chunk, to, True)
-
-        @pl.when(link == CHAIN - 1)
-        def _():
-            for to in range(CHAIN - 1):
-                send(chunk, to, False)
+                value = raw[chunk, to, time]
+                kept = value if kept is None else kept + value
+                terms = [value * table[(link * SPAN + time) * SLOW + k] for k in range(SLOW)] + [value * value]
+                moments = [term if own is None else own + term for own, term in zip(moments, terms)]
+            part[chunk, to, month] = kept
+        for k in range(SLOW + 1):
+            part[chunk, to, MONTHS + k] = moments[k]
+
+        @pl.when((link == 0) & (to > 0))
+        def _():
+            send(chunk, to, True)
+
+        @pl.when((link == CHAIN - 1) & (to < CHAIN - 1))
+        def _():
+            send(chunk, to, False)
 
     def relay(step):
         for at in range(1, CHAIN - 1):
-
-            @pl.when((link == at) & (step >= at) & (step < chunks + at))
-            def _():
-                for to in range(CHAIN - 1, at, -1):
-                    arrive(step - at, to, True)
-                    send(step - at, to, True)
-
-            lag = CHAIN - 1 - at
-
-            @pl.when((link == at) & (step >= lag) & (step < chunks + lag))
-            def _():
-                for to in range(at):
+            for to in range(CHAIN - 1, at, -1):
+                lag = CHAIN - 1 - to + at
+
+                @pl.when((link == at) & (step >= lag) & (step < chunks + lag))
+                def _():
+                    arrive(step - lag, to, True)
+                    send(step - lag, to, True)
+
+            for to in range(at):
+                lag = to + CHAIN - 1 - at
+
+                @pl.when((link == at) & (step >= lag) & (step < chunks + lag))
+                def _():
                     arrive(step - lag, to, False)
                     send(step - lag, to, False)
 
@@ -204,42 +211,32 @@
             arrive(chunk, link, False)
 
         coeffs, variance = finish([part[chunk, link, k] for k in range(SUMS)])
+        rows = pl.ds(pl.multiple_of(chunk * ROWS, ROWS), ROWS)
         for k in range(HARM):
-            done[chunk, k] = coeffs[k]
-        done[chunk, HARM] = variance
-        rows = pl.ds(pl.multiple_of(chunk * ROWS, ROWS), ROWS)
-        pltpu.make_async_copy(done.at[chunk, pl.ds(0, HARM)], coeff_out.at[:, rows, :], out_sem.at[0]).start()
-        pltpu.make_async_copy(done.at[chunk, HARM], var_out.at[rows, :], out_sem.at[1]).start()
-
-    lag = CHAIN + 1
-    lax.fori_loop(0, min(AHEAD, chunks), lambda c, _: (spread(c), 0)[1], 0)
+            coeff_out[k, rows, :] = coeffs[k]
+        var_out[rows, :] = variance
+
+    ramp = CHAIN - 1
+    lax.fori_loop(0, AHEAD, lambda step, _: (each(step, spread_block), 0)[1], 0)
 
     def body(step, carry):
-        @pl.when(step + AHEAD < chunks)
-        def _():
-            spread(step + AHEAD)
-
-        @pl.when(step < chunks)
-        def _():
-            add_up(step)
-
+        each(step + AHEAD, spread_block)
+        each(step, add_up)
         relay(step)
 
-        @pl.when(step >= lag)
-        def _():
-            close(step - lag)
+        @pl.when(step >= ramp + CLOSE_LAG)
+        def _():
+            close(step - ramp - CLOSE_LAG)
 
         return carry
 
-    lax.fori_loop(0, chunks + lag, body, 0)
+    lax.fori_loop(0, chunks + ramp + CLOSE_LAG, body, 0)
 
     lons = pl.ds(0, (members - 1) * CHAIN * LANES)
     sent = field.at[:, :, lons] if local_rows % lat == 0 else field.at[:, lons]
     pltpu.make_async_copy(sent, sent, raw_send).wait()
     passed = part.at[:, pl.ds(0, CHAIN - 1)]
     pltpu.make_async_copy(passed, passed, part_send).wait()
-    pltpu.make_async_copy(coeff_out, coeff_out, out_sem.at[0]).wait()
-    pltpu.make_async_copy(var_out, var_out, out_sem.at[1]).wait()
 
 
 def local(snapshots):
@@ -259,22 +256,20 @@
             jax.ShapeDtypeStruct((lat, LANES), jnp.float32),
         ),
         in_specs=[pl.BlockSpec(memory_space=pltpu.SMEM), pl.BlockSpec(memory_space=pl.ANY)],
-        out_specs=(pl.BlockSpec(memory_space=pl.ANY), pl.BlockSpec(memory_space=pl.ANY)),
+        out_specs=(pl.BlockSpec(memory_space=pltpu.VMEM), pl.BlockSpec(memory_space=pltpu.VMEM)),
         scratch_shapes=[
             pltpu.VMEM((chunks, CHAIN, SPAN, ROWS, LANES), jnp.float32),
             pltpu.VMEM((chunks, CHAIN, SUMS, ROWS, LANES), jnp.float32),
             pltpu.VMEM((chunks, CHAIN, SUMS, ROWS, LANES), jnp.float32),
             pltpu.VMEM((chunks, CHAIN, SUMS, ROWS, LANES), jnp.float32),
-            pltpu.VMEM((chunks, SUMS, ROWS, LANES), jnp.float32),
             pltpu.SemaphoreType.DMA,
-            pltpu.SemaphoreType.DMA((chunks,)),
+            pltpu.SemaphoreType.DMA((chunks, CHAIN)),
             pltpu.SemaphoreType.DMA,
             pltpu.SemaphoreType.DMA((chunks, CHAIN)),
             pltpu.SemaphoreType.DMA((chunks, CHAIN)),
-            pltpu.SemaphoreType.DMA((2,)),
         ],
         compiler_params=pltpu.CompilerParams(
-            collective_id=0, has_side_effects=True, vmem_limit_bytes=56 * 2**20
+            collective_id=0, has_side_effects=True, vmem_limit_bytes=44 * 2**20
         ),
         name="climatology",
     )(table, field)

time: 167 us -> 161 us (0.964)
  Pallas kernels: 159 us -> 155 us
    pallas_call x1, Pallas kernels: 159 us -> 155 us  [local(): pl.pallas_call(functools.partial(kernel, groups, lat, local_rows), out_sh...]
where the time goes in v2:
time: 161 us; the launch traced here: 159 us
  Pallas kernels  155 us (96%)
  local copies, waits for them, and re-layouts  2.65 us (2%)
    pallas_call x1, Pallas kernels, local(): pl.pallas_call(functools.partial(kernel, groups, lat, local_rows), out_sh...  155 us

profile of v2, /device:TPU:11, one launch (start us, length us, event | category | flops | bytes accessed | tf_op | source)
XLA Modules:
  0.0 158.7 jit_solution(6966547183907267804)
XLA Ops:
  0.6 0.0 copy-start
  0.6 0.7 copy-done
  1.3 155.4 %climatology.1 = (f32[16,256,128]{2,1,0:T(8,128)S(1)}, f32[256,128]{1,0:T(8,128)S(1)}) custom-call(f32[384]{0:T(512)S(1)} %copy-done, f32[6,256,2048]{2,1,0:T(8,128)} %bitcast.1), custom_call_target="tpu_custom_call" | custom-call | tf_op jit(solution)/shard_map/climatology/pallas_call | solution.py:252
  156.7 1.3 copy.6
  158.1 0.7 copy.7
Async XLA Ops:
  0.6 0.7 copy-start

commit v3 on v2

--- a/solution.py
+++ b/solution.py
@@ -73,7 +73,7 @@
 
 def kernel(
     groups, lat, local_rows,
-    table, field, coeff_out, var_out,
+    field, coeff_out, var_out,
     raw, part, below, above,
     raw_send, raw_recv, part_send, below_recv, above_recv,
 ):
@@ -82,6 +82,12 @@
     me = lax.axis_index("io")
     link, member = me // members, lax.rem(me, members)
     device = lambda at, who: {"io": at * members + who}
+
+    span = fit_constants()[0][:SPAN]
+    offset = link.astype(jnp.float32) * np.float32(SPAN / (TIMES / 2.0))
+    quarter = lambda at: (link == at).astype(jnp.float32)
+    turn_cos, turn_sin = quarter(0) - quarter(2), quarter(1) - quarter(3)
+    flip = quarter(0) - quarter(1) + quarter(2) - quarter(3)
 
     barrier = pltpu.get_barrier_semaphore()
     for step in range(1, members):
@@ -163,17 +169,23 @@
 
     def add_up(chunk, to):
         pltpu.make_async_copy(raw.at[chunk, to], raw.at[chunk, to], raw_recv.at[chunk, to]).wait()
-        moments = [None] * (SLOW + 1)
+        local = [None] * (SLOW + 1)
+        whole = None
         for month in range(MONTHS):
             kept = None
             for time in range(month, SPAN, MONTHS):
                 value = raw[chunk, to, time]
                 kept = value if kept is None else kept + value
-                terms = [value * table[(link * SPAN + time) * SLOW + k] for k in range(SLOW)] + [value * value]
-                moments = [term if own is None else own + term for own, term in zip(moments, terms)]
+                terms = [value * np.float32(span[time, k]) for k in range(SLOW)] + [value * value]
+                local = [term if own is None else own + term for own, term in zip(local, terms)]
             part[chunk, to, month] = kept
-        for k in range(SLOW + 1):
-            part[chunk, to, MONTHS + k] = moments[k]
+            whole = kept if whole is None else whole + kept
+        trend, cosine, sine, double, squares = local
+        part[chunk, to, MONTHS] = trend + whole * offset
+        part[chunk, to, MONTHS + 1] = cosine * turn_cos - sine * turn_sin
+        part[chunk, to, MONTHS + 2] = cosine * turn_sin + sine * turn_cos
+        part[chunk, to, MONTHS + 3] = double * flip
+        part[chunk, to, MONTHS + 4] = squares
 
         @pl.when((link == 0) & (to > 0))
         def _():
@@ -237,6 +249,17 @@
     pltpu.make_async_copy(sent, sent, raw_send).wait()
     passed = part.at[:, pl.ds(0, CHAIN - 1)]
     pltpu.make_async_copy(passed, passed, part_send).wait()
+
+
+def put_out(coeffs, variance, coeff_out, var_out, sem):
+    copies = [
+        pltpu.make_async_copy(coeffs, coeff_out, sem.at[0]),
+        pltpu.make_async_copy(variance, var_out, sem.at[1]),
+    ]
+    for copy in copies:
+        copy.start()
+    for copy in copies:
+        copy.wait()
 
 
 def local(snapshots):
@@ -246,16 +269,14 @@
     if width != groups * LANES or lat % ROWS or local_rows % ROWS or groups % CHAIN:
         raise ValueError("unsupported sizes")
     chunks = lat // ROWS
-    slow = fit_constants()[0]
-    table = jnp.asarray(slow.reshape(-1), jnp.float32)
     field = snapshots.reshape(local_rows // lat, lat, width) if local_rows % lat == 0 else snapshots
-    return pl.pallas_call(
+    results = pl.pallas_call(
         functools.partial(kernel, groups, lat, local_rows),
         out_shape=(
             jax.ShapeDtypeStruct((HARM, lat, LANES), jnp.float32),
             jax.ShapeDtypeStruct((lat, LANES), jnp.float32),
         ),
-        in_specs=[pl.BlockSpec(memory_space=pltpu.SMEM), pl.BlockSpec(memory_space=pl.ANY)],
+        in_specs=[pl.BlockSpec(memory_space=pl.ANY)],
         out_specs=(pl.BlockSpec(memory_space=pltpu.VMEM), pl.BlockSpec(memory_space=pltpu.VMEM)),
         scratch_shapes=[
             pltpu.VMEM((chunks, CHAIN, SPAN, ROWS, LANES), jnp.float32),
@@ -272,7 +293,16 @@
             collective_id=0, has_side_effects=True, vmem_limit_bytes=44 * 2**20
         ),
         name="climatology",
-    )(table, field)
+    )(field)
+    return pl.pallas_call(
+        put_out,
+        out_shape=tuple(jax.ShapeDtypeStruct(r.shape, r.dtype) for r in results),
+        in_specs=[pl.BlockSpec(memory_space=pltpu.VMEM)] * 2,
+        out_specs=(pl.BlockSpec(memory_space=pl.ANY),) * 2,
+        scratch_shapes=[pltpu.SemaphoreType.DMA((2,))],
+        compiler_params=pltpu.CompilerParams(vmem_limit_bytes=4 * 2**20),
+        name="put_out",
+    )(*results)
 
 
 def solution(mesh):

time: 161 us -> 159 us (0.988)
  local copies, waits for them, and re-layouts: 2.65 us -> 0 us
    unnamed x4 -> x0, local copies, waits for them, and re-layouts: 2.65 us -> none
where the time goes in v3:
time: 159 us; the launch traced here: 157 us
  Pallas kernels  156 us (98%)
    pallas_call x1, Pallas kernels, local(): pl.pallas_call(functools.partial(kernel, groups, lat, local_rows), out_sh...  155 us

profile of v3, /device:TPU:11, one launch (start us, length us, event | category | flops | bytes accessed | tf_op | source)
XLA Modules:
  0.0 156.9 jit_solution(12042988322865266141)
XLA Ops:
  0.6 154.9 %climatology.1 = (f32[16,256,128]{2,1,0:T(8,128)S(1)}, f32[256,128]{1,0:T(8,128)S(1)}) custom-call(f32[6,256,2048]{2,1,0:T(8,128)} %bitcast.1), custom_call_target="tpu_custom_call" | custom-call | tf_op jit(solution)/shard_map/climatology/pallas_call | solution.py:273
  155.5 1.4 put_out.1
